TPU v7x, 256 devices: a 8x8x2 block of a 8x8x16 slice. The times are simulated.
256 devices in a mesh: rep: 2 (over z), exp: 8 (over x), ten: 16 (over y, core).
Axes of the slice: x: 8, y: 8, z: 2, core: 2. Of those that a mesh axis runs over, the one named last changes fastest.
The devices are a block of a 8x8x16 slice.
Arguments:
- hidden_in: bfloat16 [6144, 3072], P(('rep', 'exp', 'ten')), parts along dimension 0, may hold values from -6 to 6
- queries: bfloat16 [6144, 6144], P(('rep', 'exp', 'ten')), parts along dimension 0, may hold values from -100 to 100
- new_kv: bfloat16 [2, 6144, 1024], P(None, ('rep', 'exp', 'ten')), parts along dimension 1, may hold values from -5 to 5
- prefix_kv: bfloat16 [2, 16, 512, 1024], P(None, ('rep', 'exp'), 'ten'), parts along dimension 1, may hold values from -5 to 5
- decode_kv: bfloat16 [2, 1024, 48, 1024], P(None, ('rep', 'exp', 'ten')), parts along dimension 1, may hold values from -5 to 5
- prefix_len: int32 [16], P(('rep', 'exp')), parts along dimension 0, may hold values from 2 to 512
- decode_len: int32 [1024], P(('rep', 'exp', 'ten')), parts along dimension 0, may hold values from 2 to 48
- out_proj: bfloat16 [6144, 3072], P('ten'), may hold values from -0.078125 to 0.078125
- norm_gain: float32 [3072], replicated, may hold values from 0.5 to 1.5
- router_w: bfloat16 [3072, 8], replicated, may hold values from -0.109375 to 0.109375
- expert_ids: int32 [6144, 2], P(('rep', 'exp', 'ten')), parts along dimension 0, may hold values from 0 to 7, all different within a row; in each aligned block of 24 rows (0 to 23, 24 to 47, ...) at most 7 rows name the same one
- w_gate: bfloat16 [8, 3072, 8192], P('exp', None, 'ten'), may hold values from -0.109375 to 0.109375
- w_up: bfloat16 [8, 3072, 8192], P('exp', None, 'ten'), may hold values from -0.109375 to 0.109375
- w_down: bfloat16 [8, 8192, 3072], P('exp', 'ten'), may hold values from -0.0625 to 0.0625
Outputs:
- layer_out: bfloat16 [6144, 3072], P(('rep', 'exp', 'ten')), parts along dimension 0
There are 2 independent parts, one for each index of `rep`. A program takes and returns all parts, laid end to end along the dimension named above; an argument that names none is the same for every part. Nothing has to cross between parts.
Inputs may be any that keep to these rules, and one draw needn't show every extreme that they name: `expert_ids`: each row names two different experts. Within each aligned block of 24 rows (the rows of one device) no expert is named by more than 7 rows, and in some block one expert is named by exactly 7 rows.
All inputs are finite; a program needn't handle non-finite values.
Results may differ from a plain program's by a relative error of at most 0.013.
Values may be sent and summed in bfloat16 or wider, within the bound.
A program may use at most 128 MiB of HBM per device.

v0:
```python
import jax
import jax.numpy as jnp
from jax import lax
from jax.experimental import pallas as pl
from jax.experimental.pallas import tpu as pltpu
from jax.sharding import Mesh
from jax.sharding import PartitionSpec as P

MESH = pl.DeviceIdType.MESH
HD = 128
CAP = 7
F32 = jnp.float32
BF16 = jnp.bfloat16
NEG = -1e30
CHUNKS = 6
RING_WIRE, RING_TURN, RING_SPREAD = 1.25, 2.2, 4.5
EXP, CHIP, CORE = "exp", "ten_0", "ten_1"
TEN = (CHIP, CORE)
REP_EXP_TEN = ("rep", EXP, CHIP, CORE)


def iota(shape, dim):
    return lax.broadcasted_iota(jnp.int32, shape, dim)


def cols(start, size):
    return pl.ds(pl.multiple_of(start, 128), size)


def rows(start, size, align):
    return pl.ds(pl.multiple_of(start, align), size)


def dot(a, b):
    return jnp.dot(a, b, preferred_element_type=F32)


def dot_t(a, b):
    return lax.dot_general(a, b, (((1,), (1,)), ((), ())), preferred_element_type=F32)


def ring_order(chips):
    far = chips // 2
    order = []
    for hop in range(far - 1, 0, -1):
        order += [(False, hop), (True, hop + 1)]
    return order + [(True, 1)]


def ring_schedule(chips, subs, wire, turn, spread):
    order = ring_order(chips)
    place = {m: i for i, m in enumerate(order)}
    arrive, clock = {}, 0.0
    for index in (0, 1):
        for sub in range(subs):
            clock += wire
            arrive[index, sub] = clock + turn
    waiting = [(index, sub) for index in range(2, len(order)) for sub in range(subs)]
    steps = []
    while waiting:
        ready = {
            (index, sub): arrive.get((place[order[index][0], order[index][1] + 1], sub), 1e9)
            for index, sub in waiting
        }
        clock = max(clock, min(ready.values()))
        due = {m: spread * m[1] - order[m[0]][1] * (wire + turn) for m in waiting if ready[m] <= clock}
        pick = min(due, key=lambda m: (due[m], m))
        waiting.remove(pick)
        steps.append((clock, 0) + pick)
        clock += wire
        arrive[pick] = clock + turn
    last = [place[True, 1], place[False, 1]]
    for sub in range(subs):
        steps.append((max(arrive[i, sub] for i in last), 1, 0, sub))
    return [step[1:] for step in sorted(steps)]


def near_first(n):
    return [(o + 1) // 2 if o % 2 else n - o // 2 for o in range(1, n)]


def ring_turns(chips):
    far = chips // 2
    return [far] + [o for d in range(far - 1, 0, -1) for o in (d, chips - d)] + [0]


class Copies:
    def __init__(self):
        self.kinds = []

    def start(self, copy):
        copy.start()
        return copy

    def sent(self, whole, sem):
        self.kinds.append((whole, sem))

    def drain(self):
        for whole, sem in self.kinds:
            arrived(whole, sem)


def arrived(whole, sem):
    pltpu.make_async_copy(whole, whole, sem).wait()


def remote(src, dst, send_sem, recv_sem, **device):
    return pltpu.make_async_remote_copy(
        src_ref=src, dst_ref=dst, send_sem=send_sem, recv_sem=recv_sem,
        device_id=device, device_id_type=MESH,
    )


class RingSum:
    def __init__(self, y, chips, copies, part, out, into, s_sem, r_sem, subs):
        self.y, self.chips, self.copies, self.part = y, chips, copies, part
        self.out, self.into, self.s_sem, self.r_sem, self.subs = out, into, s_sem, r_sem, subs
        self.order = ring_order(chips)
        self.place = {m: i for i, m in enumerate(self.order)}
        copies.sent(out, s_sem.at[0])

    def first(self, index, sub, way, before=None):
        is_long, hop = self.order[index]
        value = self.part(hop if way == 0 else self.chips - hop, (0 if is_long else 1) ^ way, sub)
        if before is not None:
            value = value + self.into[way, before, sub].astype(F32)
        self.out[way, index, sub] = value.astype(BF16)
        to = lax.rem(self.y + (1 if way == 0 else self.chips - 1), self.chips)
        self.copies.start(remote(
            self.out.at[way, index, sub], self.into.at[way, index, sub],
            self.s_sem.at[0], self.r_sem.at[index, sub], **{CHIP: to},
        ))

    def wait(self, index, sub):
        arrived(self.into.at[:, index, sub], self.r_sem.at[index, sub])

    def send(self, index, sub):
        is_long, hop = self.order[index]
        before = self.place[is_long, hop + 1]
        self.wait(before, sub)
        for way in range(2):
            self.first(index, sub, way, before)

    def totals(self, sub):
        last = [self.place[True, 1], self.place[False, 1]]
        for index in last:
            self.wait(index, sub)
        return [
            self.part(0, half, sub)
            + self.into[0, last[half], sub].astype(F32)
            + self.into[1, last[1 - half], sub].astype(F32)
            for half in range(2)
        ]


def k1_scratch(d):
    r, c, n = d["rows"], d["chips"], 2 * d["chips"]
    jw = d["heads_dev"] * HD
    half = d["model"] // 2
    msgs = len(ring_order(c))
    v, dma = pltpu.VMEM, pltpu.SemaphoreType.DMA
    return dict(
        q_v=v((r, d["heads_q"] * HD), BF16),
        nkv_v=v((2, r, d["kvw"]), BF16),
        pre_v=v((2, d["pre_dev"], d["kvw"]), BF16),
        dec_v=v((2, d["dec"], d["ctx"], d["kvw"]), BF16),
        qb=v((n, r, jw), BF16),
        kvn=v((2, c, 2, r, HD), BF16),
        kvp=v((2, c, 2, d["pre_dev"], HD), BF16),
        dec_o=v((d["heads_q"] * 8, HD), BF16),
        decs=v((n, 16, HD), BF16),
        decr=v((n, 16, HD), BF16),
        qh=v((d["heads_dev"] * n * r, HD), BF16),
        kall=v((n * (d["pre_dev"] + r), HD), BF16),
        vall=v((n * (d["pre_dev"] + r), HD), BF16),
        att=v((n * r, 2 * jw), BF16),
        wo=v((2 * jw, half), BF16),
        part=v((n * r, half), F32),
        rs_out=v((2, msgs, CHUNKS // 2, 2 * r, half // CHUNKS), BF16),
        rs_in=v((2, msgs, CHUNKS // 2, 2 * r, half // CHUNKS), BF16),
        l_sem=dma((8,)),
        qs_sem=dma((1,)),
        qr_sem=dma((1,)),
        kns_sem=dma((1,)),
        knr_sem=dma((1,)),
        kps_sem=dma((1,)),
        kpr_sem=dma((1,)),
        x_s=dma((5,)),
        x_r=dma((5,)),
        ds_sem=dma((1,)),
        dr_sem=dma((1,)),
        rs_s=dma((1,)),
        rs_r=dma((msgs, CHUNKS // 2)),
    )


def attend_and_project(d, S, y, k, copies, q_hbm, nkv_hbm, pre_hbm, dec_hbm, plen, dlen, wo_hbm, barrier, then):
    r, c, n, dec, span = d["rows"], d["chips"], 2 * d["chips"], d["dec"], d["rows"] - d["dec"]
    hq, per_kv, hd_dev, ctx, pre_dev = d["heads_q"], d["per_kv"], d["heads_dev"], d["ctx"], d["pre_dev"]
    jw, half = hd_dev * HD, d["model"] // 2
    t = 2 * y + k
    other = 1 - k
    scale = HD ** -0.5
    l_sem = S["l_sem"]

    def local(src, dst, i):
        copy = pltpu.make_async_copy(src, dst, l_sem.at[i])
        copy.start()
        return copy

    kv_cols = cols(y * HD, HD)
    l_n = local(nkv_hbm, S["nkv_v"], 0)
    l_p = local(pre_hbm.at[:, 0], S["pre_v"], 1)
    l_q = local(q_hbm, S["q_v"], 2)
    l_own = [
        local(nkv_hbm.at[:, :, kv_cols], S["kvn"].at[k, y], 3),
        local(pre_hbm.at[:, 0, :, kv_cols], S["kvp"].at[k, y], 4),
        local(q_hbm.at[:, cols(t * jw, jw)], S["qb"].at[t], 5),
    ]
    l_d = local(dec_hbm, S["dec_v"], 6)
    l_w = local(wo_hbm.at[:, cols(k * half, half)], S["wo"].at[rows(k * jw, jw, 16)], 7)

    barrier()

    def kn_copy(src_y, to):
        return remote(
            S["nkv_v"].at[:, :, cols(to * HD, HD)], S["kvn"].at[k, src_y],
            S["kns_sem"].at[0], S["knr_sem"].at[0], **{CHIP: to},
        )

    def kp_copy(src_y, to):
        return remote(
            S["pre_v"].at[:, :, cols(to * HD, HD)], S["kvp"].at[k, src_y],
            S["kps_sem"].at[0], S["kpr_sem"].at[0], **{CHIP: to},
        )

    def q_copy(src_t, to_t):
        return remote(
            S["q_v"].at[:, cols(to_t * jw, jw)], S["qb"].at[src_t],
            S["qs_sem"].at[0], S["qr_sem"].at[0], **{CHIP: to_t // 2, CORE: to_t % 2},
        )

    l_n.wait()
    l_p.wait()
    for o in near_first(c)[::-1]:
        to = lax.rem(y + o, c)
        copies.start(kn_copy(y, to))
        copies.start(kp_copy(y, to))
    wo_copy = copies.start(remote(
        wo_hbm.at[:, cols(other * half, half)], S["wo"].at[rows(k * jw, jw, 16)], S["x_s"].at[0], S["x_r"].at[0],
        **{CORE: other},
    ))
    then()

    l_q.wait()
    l_d.wait()
    q8 = S["q_v"][16:24, :].astype(F32)
    n8 = [S["nkv_v"][i, 16:24, :].astype(F32) for i in range(2)]
    m = per_kv * 8
    keys = dec * ctx
    lane = iota((m, keys), 1)
    row8 = iota((m, keys), 0) & 7
    req = sum((lane >= ctx * i).astype(jnp.int32) for i in range(1, dec))
    pos = lane - ctx * req
    length = dlen[0]
    for i in range(1, dec):
        length = jnp.where(req == i, dlen[i], length)
    seen = (row8 - (8 - dec) == req) & (pos < length)
    for g in range(hq // per_kv):
        qg = jnp.concatenate(
            [q8[:, (g * per_kv + h) * HD : (g * per_kv + h + 1) * HD] for h in range(per_kv)], axis=0
        )
        kg = S["dec_v"][0, :, :, g * HD : (g + 1) * HD].reshape(keys, HD)
        vg = S["dec_v"][1, :, :, g * HD : (g + 1) * HD].reshape(keys, HD)
        own_k = jnp.concatenate([n8[0][:, g * HD : (g + 1) * HD]] * per_kv, axis=0)
        own_v = jnp.concatenate([n8[1][:, g * HD : (g + 1) * HD]] * per_kv, axis=0)
        s = jnp.where(seen, dot_t(qg.astype(BF16), kg) * scale, NEG)
        s_own = jnp.sum(qg * own_k, axis=1, keepdims=True) * scale
        top = jnp.maximum(jnp.max(s, axis=1, keepdims=True), s_own)
        p = jnp.where(seen, jnp.exp(s - top), 0.0)
        p_own = jnp.exp(s_own - top)
        den = jnp.sum(p, axis=1, keepdims=True) + p_own
        o = dot(p.astype(BF16), vg) + p_own.astype(BF16).astype(F32) * own_v
        S["dec_o"][g * m : (g + 1) * m, :] = (o / den).astype(BF16)
    to_row = iota((n * 16, hq * 8), 0)
    from_row = iota((n * 16, hq * 8), 1)
    slot = to_row & 15
    wanted = (to_row >> 4) * (8 * hd_dev) + (slot >> 2) * 8 + (8 - dec) + (slot & 3)
    pick = ((from_row == wanted) & (slot < hd_dev * dec)).astype(BF16)
    S["decs"][...] = dot(pick, S["dec_o"][...]).astype(BF16).reshape(n, 16, HD)

    def d_copy(src_t, to_t):
        return remote(
            S["decs"].at[to_t], S["decr"].at[src_t],
            S["ds_sem"].at[0], S["dr_sem"].at[0], **{CHIP: to_t // 2, CORE: to_t % 2},
        )

    for o in range(n - 1, 0, -1):
        copies.start(d_copy(t, lax.rem(t + o, n)))
    S["decr"][t] = S["decs"][t]
    for o in near_first(c)[::-1] + [0]:
        to = lax.rem(y + o, c)
        for kk in ([1] if o == 0 else [0, 1]):
            copies.start(q_copy(t, 2 * to + lax.rem(k + kk, 2)))

    for copy in l_own:
        copy.wait()
    arrived(S["kvn"].at[k, : c - 1], S["knr_sem"].at[0])
    arrived(S["kvp"].at[k, : c - 1], S["kpr_sem"].at[0])
    copies.sent(S["kvn"].at[k, : c - 1], S["kns_sem"].at[0])
    copies.sent(S["kvp"].at[k, : c - 1], S["kps_sem"].at[0])
    copies.sent(S["qb"].at[: n - 1], S["qs_sem"].at[0])
    copies.sent(S["decs"].at[: n - 1], S["ds_sem"].at[0])
    relay = [
        copies.start(remote(S[b].at[k], S[b].at[k], S["x_s"].at[i], S["x_r"].at[i], **{CORE: other}))
        for i, b in ((1, "kvn"), (2, "kvp"))
    ]
    arrived(S["qb"].at[: n - 1], S["qr_sem"].at[0])
    turn = ring_turns(c)
    chip_at = [lax.rem(y + o, c) for o in turn]
    for cc in range(c):
        pair = [S["qb"][2 * chip_at[cc] + i].astype(F32) for i in range(2)]
        for j in range(hd_dev):
            S["qh"][j * n * r + cc * 2 * r : j * n * r + (cc + 1) * 2 * r, :] = jnp.concatenate(
                [q[:, j * HD : (j + 1) * HD] for q in pair], axis=0
            ).astype(BF16)
    for copy in relay:
        copy.wait()
    prefix = n * pre_dev
    for i, b in ((0, "kall"), (1, "vall")):
        for cc in range(c):
            for kk in range(2):
                at = (2 * cc + kk) * pre_dev
                S[b][at : at + pre_dev, :] = S["kvp"][kk, cc, i]
            S[b][prefix + cc * 2 * r : prefix + (cc + 1) * 2 * r, :] = jnp.concatenate(
                [S["kvn"][kk, cc, i].astype(F32) for kk in range(2)], axis=0
            ).astype(BF16)
    arrived(S["decr"].at[: n - 1], S["dr_sem"].at[0])

    block_devs = 8
    block = block_devs * r
    col = iota((1, n * r), 1)
    col_dev = sum((col >= r * i).astype(jnp.int32) for i in range(1, n))
    col_in = col - r * col_dev
    key_place = jnp.where(col_in < span, col_dev * span + col_in, 1 << 20)
    pre_seen = iota((1, prefix), 1) < plen[0]
    row = iota((block, 1), 0)
    row_dev = sum((row >= r * i).astype(jnp.int32) for i in range(1, block_devs))
    row_in = row - r * row_dev
    from_col = iota((block, n * 16), 1)
    att_copies = []
    for b in range(n // block_devs):
        chip = sum(
            jnp.where((row_dev >> 1) == i, chip_at[b * block_devs // 2 + i], 0) for i in range(block_devs // 2)
        )
        device = 2 * chip + (row_dev & 1)
        new_seen = key_place <= device * span + row_in
        first = b * block
        for j in range(hd_dev):
            q = S["qh"][j * n * r + first : j * n * r + first + block, :]
            s1 = jnp.where(pre_seen, dot_t(q, S["kall"][:prefix, :]), NEG)
            s2 = jnp.where(new_seen, dot_t(q, S["kall"][prefix:, :]), NEG)
            top = jnp.maximum(jnp.max(s1, axis=1, keepdims=True), jnp.max(s2, axis=1, keepdims=True))
            p1 = jnp.exp((s1 - top) * scale)
            p2 = jnp.exp((s2 - top) * scale)
            den = jnp.sum(p1, axis=1, keepdims=True) + jnp.sum(p2, axis=1, keepdims=True)
            o = (dot(p1.astype(BF16), S["vall"][:prefix, :]) + dot(p2.astype(BF16), S["vall"][prefix:, :])) / den
            wanted = jnp.where(row_in >= span, device * 16 + j * dec + row_in - span, -1)
            own = dot((from_col == wanted).astype(BF16), S["decr"][...].reshape(n * 16, HD))
            S["att"][first : first + block, cols(k * jw + j * HD, HD)] = jnp.where(
                row_in < span, o, own
            ).astype(BF16)
        view = S["att"].at[first : first + block, cols(k * jw, jw)]
        att_copies.append(copies.start(remote(
            view, view, S["x_s"].at[3 + b], S["x_r"].at[3 + b], **{CORE: other},
        )))
    l_w.wait()
    wo_copy.wait()

    width, subs = half // CHUNKS, CHUNKS // 2
    row_of = {o: i * 2 * r for i, o in enumerate(turn)}

    def share(o, h, sub):
        first = (h * subs + sub) * width
        return S["part"][row_of[o] : row_of[o] + 2 * r, first : first + width]

    ring = RingSum(y, c, copies, share, S["rs_out"], S["rs_in"], S["rs_s"], S["rs_r"], subs)
    for b, copy in enumerate(att_copies):
        copy.wait()
        these = slice(b * block, (b + 1) * block)
        for sub in range(subs):
            for h in range(2):
                first = (h * subs + sub) * width
                S["part"][these, first : first + width] = dot(
                    S["att"][these, :], S["wo"][:, first : first + width]
                )
                if b == 0:
                    ring.first(0, sub, 1 - h)
                    ring.first(1, sub, h)
    for index in range(2, len(ring.order)):
        for sub in range(subs):
            ring.send(index, sub)
    sums = [ring.totals(sub) for sub in range(subs)]
    return [sums[sub][h] for h in range(2) for sub in range(subs)]


def entry_barrier(y, k, chips, x=None, groups=0):
    def greet():
        barrier = pltpu.get_barrier_semaphore()
        for o in range(chips):
            for kk in ([1] if o == 0 else [0, 1]):
                pl.semaphore_signal(
                    barrier, inc=1,
                    device_id={CHIP: lax.rem(y + o, chips), CORE: lax.rem(k + kk, 2)},
                    device_id_type=MESH,
                )
        for o in range(1, groups):
            pl.semaphore_signal(
                barrier, inc=1, device_id={EXP: lax.rem(x + o, groups)}, device_id_type=MESH
            )
        pl.semaphore_wait(barrier, 2 * chips - 1 + max(groups - 1, 0))

    return greet


def moe_scratch(d):
    r, c, groups, model, ff = d["rows"], d["chips"], d["groups"], d["model"], d["ff_dev"]
    half, slots, take = model // 2, 16, 2 * CAP
    far, nq, msgs = c // 2, CHUNKS, len(ring_order(c))
    v, dma = pltpu.VMEM, pltpu.SemaphoreType.DMA
    return dict(
        ids_v=v((2, r), jnp.int32),
        gain_v=v((1, model), F32),
        router_v=v((d["experts"], model), BF16),
        ids_b=v((2, r, 128), jnp.int32),
        hin=v((2, r, half), BF16),
        res=v((2 * r, half), F32),
        stat=v((2, 2 * r, 128), F32),
        pick=v((2, 2 * r, 128), F32),
        normed=v((2 * r, half), BF16),
        wg=v((model, ff), BF16),
        wu=v((model, ff), BF16),
        wd=v((2, ff, half), BF16),
        xs=v((groups, slots, half), BF16),
        xr=v((groups, slots, half), BF16),
        xg=v((2, c, groups * take, half), BF16),
        hid=v((2, c * groups * take, ff), BF16),
        part2=v((c * groups * take, half), F32),
        rs2_out=v((2, msgs, nq // 2, groups * take, half // nq), BF16),
        rs2_in=v((2, msgs, nq // 2, groups * take, half // nq), BF16),
        ys=v((groups, slots, half), BF16),
        yr=v((groups, slots, half), BF16),
        fin=v((2, 2 * r, half), F32),
        m_l=dma((8,)),
        m_s=dma((5,)),
        m_r=dma((5,)),
        xs_s=dma((1,)),
        xs_r=dma((nq,)),
        ag_s=dma((1,)),
        ag_r=dma((far, nq)),
        pc_s=dma((1,)),
        pc_r=dma((far + 1,)),
        h_s=dma((1,)),
        h_r=dma((far + 1,)),
        rs2_s=dma((1,)),
        rs2_r=dma((msgs, nq // 2)),
        ys_s=dma((1,)),
        ys_r=dma((nq,)),
        f_s=dma((1,)),
        f_r=dma((1,)),
    )


class Experts:
    def __init__(self, d, S, x, y, k, copies, hidden_hbm, ids, gain, router_t, wg_hbm, wu_hbm, wd_hbm, out):
        self.d, self.S, self.x, self.y, self.k, self.copies = d, S, x, y, k, copies
        self.hidden_hbm, self.ids, self.gain, self.router_t = hidden_hbm, ids, gain, router_t
        self.wg_hbm, self.wu_hbm, self.wd_hbm, self.out = wg_hbm, wu_hbm, wd_hbm, out

    def early(self):
        self.ids_load = pltpu.make_async_copy(self.ids, self.S["ids_v"], self.S["m_l"].at[4])
        self.ids_load.start()

    def load(self):
        S, k, d = self.S, self.k, self.d
        half, other = d["model"] // 2, 1 - self.k
        r = d["rows"]
        self.ids_load.wait()
        one = (iota((r, r), 0) == iota((r, r), 1)).astype(BF16)
        ids = dot_t(one, S["ids_v"][...].astype(F32).astype(BF16)).astype(jnp.int32)
        lane = iota((r, 128), 1)
        S["ids_b"][k] = jnp.where(lane < 64, ids[:, 0:1], ids[:, 1:2])

        def exchange(src, dst, i):
            return self.copies.start(remote(src, dst, S["m_s"].at[i], S["m_r"].at[i], **{CORE: other}))

        self.ids_copy = exchange(S["ids_b"].at[k], S["ids_b"].at[k], 0)
        self.hin_copy = exchange(self.hidden_hbm.at[:, cols(other * half, half)], S["hin"].at[k], 1)
        self.wd_copy = exchange(self.wd_hbm.at[0, :, cols(other * half, half)], S["wd"].at[k], 2)
        self.exchange = exchange
        self.loads = []
        for i, (src, dst) in enumerate((
            (self.hidden_hbm.at[:, cols(k * half, half)], S["hin"].at[k]),
            (self.wg_hbm.at[0], S["wg"]),
            (self.wu_hbm.at[0], S["wu"]),
            (self.wd_hbm.at[0, :, cols(k * half, half)], S["wd"].at[k]),
            (self.gain, S["gain_v"]),
            (self.router_t, S["router_v"]),
        )):
            copy = pltpu.make_async_copy(src, dst, S["m_l"].at[i if i < 4 else i + 1])
            copy.start()
            self.loads.append(copy)

    def away(self, o):
        return min(o, self.d["chips"] - o)

    def chip(self, o):
        return self.y if o == 0 else lax.rem(self.y + o, self.d["chips"])

    def route(self):
        S, d = self.S, self.d
        r = d["rows"]
        self.ids_copy.wait()
        ids = S["ids_b"][...].reshape(2 * r, 128)
        lane, row = iota((2 * r, 128), 1), iota((2 * r, 128), 0)
        expert, slot = lane >> 4, lane & 15
        self.first = ids[:, 0:1] == expert
        hot = self.first | (ids[:, 64:65] == expert)
        a, b = iota((2 * r, 2 * r), 0), iota((2 * r, 2 * r), 1)
        below = ((b < a) & ((a < r) == (b < r))).astype(BF16)
        rank = dot(below, hot.astype(BF16)).astype(jnp.int32) + jnp.where(row < r, 0, CAP)
        self.placed = hot & (rank == slot)
        one = (iota((128, 128), 0) == iota((128, 128), 1)).astype(BF16)
        self.to_slots = dot_t(one, self.placed.astype(BF16)).astype(BF16)
        self.ids2 = ids
        self.hin_copy.wait()
        for i in (0, 4, 5):
            self.loads[i].wait()

    def ffn_gate_up(self, offs, tile):
        S, d = self.S, self.d
        half, n = d["model"] // 2, d["groups"] * 2 * CAP
        width = d["ff_dev"] // 2
        at = slice(tile * width, (tile + 1) * width)
        xh = [jnp.concatenate([S["xg"][h, self.chip(o)] for o in offs], axis=0) for h in range(2)]
        gate = dot(xh[0], S["wg"][:half, at]) + dot(xh[1], S["wg"][half:, at])
        up = dot(xh[0], S["wu"][:half, at]) + dot(xh[1], S["wu"][half:, at])
        act = (gate / (1.0 + jnp.exp(-gate)) * up).astype(BF16)
        for i, o in enumerate(offs):
            S["hid"][self.k, rows(self.chip(o) * n, n, 16), at] = act[i * n : (i + 1) * n]

    def hid_copy(self, o):
        n = self.d["groups"] * 2 * CAP
        view = self.S["hid"].at[self.k, rows(self.chip(o) * n, n, 16)]
        return remote(view, view, self.S["h_s"].at[0], self.S["h_r"].at[self.away(o)], **{CORE: 1 - self.k})

    def ffn_down(self, offs, after=None):
        S, d = self.S, self.d
        half, n = d["model"] // 2, d["groups"] * 2 * CAP
        lhs = [
            jnp.concatenate([S["hid"][h, rows(self.chip(o) * n, n, 16), :] for o in offs], axis=0)
            for h in range(2)
        ]

        def tile(at):
            value = dot(lhs[0], S["wd"][0, :, at]) + dot(lhs[1], S["wd"][1, :, at])
            for j, o in enumerate(offs):
                S["part2"][rows(self.chip(o) * n, n, 16), at] = value[j * n : (j + 1) * n]

        def step(i, carry):
            tile(cols(i * 256, 256))
            return carry

        width, subs = half // CHUNKS, CHUNKS // 2
        if after is None:
            lax.fori_loop(0, half // 256, step, 0)
        else:
            for sub in range(subs):
                for h in range(2):
                    first = (h * subs + sub) * width
                    tile(slice(first, first + width))
                    after(h, sub)

    def ffn(self, offs, stage, after=None):
        if stage == 0:
            arrived(self.S["xg"].at[0, : len(offs)], self.S["pc_r"].at[self.away(offs[0])])
            self.ffn_gate_up(offs, 0)
        elif stage == 1:
            self.ffn_gate_up(offs, 1)
            for o in offs:
                self.copies.start(self.hid_copy(o))
        elif stage == CHUNKS - 1:
            n = self.d["groups"] * 2 * CAP
            arrived(self.S["hid"].at[0, : len(offs) * n], self.S["h_r"].at[self.away(offs[0])])
            self.ffn_down(offs, after)

    def chunk(self, q):
        w = self.d["model"] // 2 // CHUNKS
        return slice(q * w, (q + 1) * w)

    def partner_copy(self, o, q):
        S = self.S
        view = S["xg"].at[self.k, self.chip(o), :, self.chunk(q)]
        return remote(view, view, S["pc_s"].at[0], S["pc_r"].at[self.away(o)], **{CORE: 1 - self.k})

    def hops(self, way, q):
        far = self.d["chips"] // 2
        return far if ((q // (CHUNKS // 2)) ^ way) == 0 else far - 1

    def gather_copy(self, way, hop, q):
        S, c = self.S, self.d["chips"]
        back = hop - 1
        src = self.chip((c - back) % c if way == 0 else back % c)
        to = self.chip(1 if way == 0 else c - 1)
        view = S["xg"].at[self.k, src, :, self.chunk(q)]
        return remote(view, view, S["ag_s"].at[0], S["ag_r"].at[hop - 1, q], **{CHIP: to})

    def swap(self, send, recv, s_sem, r_sem, src_x, to_x, q):
        S = self.S
        return remote(
            S[send].at[to_x, :, self.chunk(q)], S[recv].at[src_x, :, self.chunk(q)],
            S[s_sem].at[0], S[r_sem].at[q], **{EXP: to_x},
        )

    def run(self, totals):
        S, d, x, y, k, copies = self.S, self.d, self.x, self.y, self.k, self.copies
        r, c, groups, model = d["rows"], d["chips"], d["groups"], d["model"]
        half, far, n = model // 2, c // 2, groups * 2 * CAP
        w = half // CHUNKS
        res = S["hin"][...].astype(F32).reshape(2 * r, half) + jnp.concatenate(totals, axis=1)
        S["res"][...] = res
        S["stat"][k] = jnp.broadcast_to(jnp.sum(res * res, axis=1, keepdims=True), (2 * r, 128))
        stat_copy = self.exchange(S["stat"].at[k], S["stat"].at[k], 3)
        stat_copy.wait()
        mean = (S["stat"][0][:, 0:1] + S["stat"][1][:, 0:1]) / model
        gain = S["gain_v"][:, cols(k * half, half)]
        S["normed"][...] = (S["res"][...] * lax.rsqrt(mean + 1e-05) * gain).astype(BF16)

        near = [lax.rem(x + o, groups) for o in near_first(groups)[::-1]]
        for q in range(CHUNKS):
            at = self.chunk(q)
            S["xs"][:, :, at] = dot(self.to_slots, S["normed"][:, at]).astype(BF16).reshape(groups, 16, w)
            for to in near:
                copies.start(self.swap("xs", "xr", "xs_s", "xs_r", x, to, q))
        S["xr"][x] = S["xs"][x]
        normed = S["normed"][...]
        logits = dot_t(normed, S["router_v"][:, cols(k * half, half)])
        e8 = iota(logits.shape, 1)
        ids = self.ids2
        lane = iota((2 * r, 128), 1)
        chosen = [
            jnp.sum(jnp.where(e8 == ids[:, 64 * i : 64 * i + 1], logits, 0.0), axis=1, keepdims=True)
            for i in range(2)
        ]
        S["pick"][k] = jnp.where(lane < 64, chosen[0], chosen[1])
        pick_copy = self.exchange(S["pick"].at[k], S["pick"].at[k], 4)

        ja, jb = iota((n, 128), 1), iota((n, 128), 0)
        dense = (((ja >> 4) * (2 * CAP) + (ja & 15) == jb) & ((ja & 15) < 2 * CAP)).astype(BF16)
        def pass_on(hop, q):
            ways = [way for way in range(2) if hop <= self.hops(way, q)]
            arrived(S["xg"].at[k, : len(ways), :, self.chunk(q)], S["ag_r"].at[hop - 1, q])
            for way in ways:
                if hop < self.hops(way, q):
                    copies.start(self.gather_copy(way, hop + 1, q))
            for way in ways:
                copies.start(self.partner_copy(c - hop if way == 0 else hop, q))

        ahead = 2
        for q in range(CHUNKS):
            at = self.chunk(q)
            arrived(S["xr"].at[: groups - 1, :, at], S["xs_r"].at[q])
            S["xg"][k, y, :, at] = dot(dense, S["xr"][:, :, at].reshape(groups * 16, w)).astype(BF16)
            for way in range(2):
                copies.start(self.gather_copy(way, 1, q))
            copies.start(self.partner_copy(0, q))
            if q >= ahead:
                pass_on(1, q - ahead)
        for load in self.loads[1:4]:
            load.wait()
        self.wd_copy.wait()

        quarter, subs = half // CHUNKS, CHUNKS // 2

        def share(o, h, sub):
            first = (h * subs + sub) * quarter
            return S["part2"][rows(self.chip(o) * n, n, 16), first : first + quarter]

        ring = RingSum(y, c, copies, share, S["rs2_out"], S["rs2_in"], S["rs2_s"], S["rs2_r"], subs)
        blocks = [[0]] + [[c - s, s] for s in range(1, far)] + [[far]]
        for hop in range(1, far + 1):
            for q in range(CHUNKS):
                if hop > 1 or q >= CHUNKS - ahead:
                    pass_on(hop, q)
                self.ffn(
                    blocks[hop - 1], q, None if hop < far else lambda h, sub: ring.first(0, sub, 1 - h)
                )
        for stage in range(CHUNKS):
            self.ffn(blocks[far], stage, lambda h, sub: ring.first(1, sub, h))

        pick_copy.wait()
        l0 = S["pick"][0][:, 0:1] + S["pick"][1][:, 0:1]
        l1 = S["pick"][0][:, 64:65] + S["pick"][1][:, 64:65]
        top = jnp.maximum(l0, l1)
        e0, e1 = jnp.exp(l0 - top), jnp.exp(l1 - top)
        weight = jnp.where(self.placed, jnp.where(self.first, e0, e1) / (e0 + e1), 0.0)
        w_hi = weight.astype(BF16)
        w_lo = (weight - w_hi.astype(F32)).astype(BF16)
        ja, jb = iota((128, n), 0), iota((128, n), 1)
        spread = (((ja >> 4) * (2 * CAP) + (ja & 15) == jb) & ((ja & 15) < 2 * CAP)).astype(BF16)
        for kind, index, sub in ring_schedule(c, subs, RING_WIRE, RING_TURN, RING_SPREAD):
            if kind == 0:
                ring.send(index, sub)
                continue
            for h, value in enumerate(ring.totals(sub)):
                q = h * subs + sub
                at = self.chunk(q)
                S["ys"][:, :, at] = dot(spread, value.astype(BF16)).astype(BF16).reshape(groups, 16, w)
                for to in near:
                    copies.start(self.swap("ys", "yr", "ys_s", "ys_r", x, to, q))
        S["yr"][x] = S["ys"][x]

        def back(q):
            view = S["fin"].at[k, rows((1 - k) * r, r, 8), self.chunk(q)]
            return remote(view, view, S["f_s"].at[0], S["f_r"].at[0], **{CORE: 1 - k})

        for q in [h * subs + sub for sub in range(subs) for h in range(2)]:
            at = self.chunk(q)
            arrived(S["yr"].at[: groups - 1, :, at], S["ys_r"].at[q])
            got = S["yr"][:, :, at].reshape(groups * 16, w)
            S["fin"][k, :, at] = S["res"][:, at] + dot(w_hi, got) + dot(w_lo, got)
            copies.start(back(q))
        arrived(S["fin"].at[1 - k, rows(k * r, r, 8), :], S["f_r"].at[0])
        for h in range(2):
            self.out[:, h * half : (h + 1) * half] = S["fin"][h, rows(k * r, r, 8), :].astype(BF16)
        copies.sent(S["xs"].at[: groups - 1], S["xs_s"].at[0])
        copies.sent(S["ys"].at[: groups - 1], S["ys_s"].at[0])
        copies.sent(S["xg"].at[0, : c - 1], S["ag_s"].at[0])
        copies.sent(S["xg"].at[0], S["pc_s"].at[0])
        copies.sent(S["hid"].at[0], S["h_s"].at[0])
        copies.sent(S["fin"].at[k, rows((1 - k) * r, r, 8), :], S["f_s"].at[0])


def on_device(
    hidden_in,
    queries,
    new_kv,
    prefix_kv,
    decode_kv,
    prefix_len,
    decode_len,
    out_proj,
    norm_gain,
    router_w,
    expert_ids,
    w_gate,
    w_up,
    w_down,
):
    chips, hq, kvw = lax.axis_size(CHIP), queries.shape[1] // HD, new_kv.shape[2]
    d = dict(
        rows=hidden_in.shape[0], model=hidden_in.shape[1], kvw=kvw, chips=chips, heads_q=hq,
        per_kv=hq // (kvw // HD), heads_dev=hq // (2 * chips), pre_dev=prefix_kv.shape[2],
        dec=decode_len.shape[0], ctx=decode_kv.shape[2], groups=lax.axis_size(EXP), ff_dev=w_gate.shape[2],
        experts=router_w.shape[1],
    )
    scratch = {**k1_scratch(d), **moe_scratch(d)}
    names = list(scratch)

    def kernel(q, nkv, pre, dec, plen, dlen, wo, hid, ids, gain, router, wg, wu, wd, out, *rest):
        S = dict(zip(names, rest))
        x, y, k = lax.axis_index(EXP), lax.axis_index(CHIP), lax.axis_index(CORE)
        copies = Copies()
        experts = Experts(d, S, x, y, k, copies, hid, ids, gain, router, wg, wu, wd, out)
        experts.early()
        totals = attend_and_project(
            d, S, y, k, copies, q, nkv, pre, dec, plen, dlen, wo,
            entry_barrier(y, k, chips, x, d["groups"]), experts.load,
        )
        experts.route()
        experts.run(totals)
        copies.drain()

    anys = pl.BlockSpec(memory_space=pl.ANY)
    smem = pl.BlockSpec(memory_space=pltpu.SMEM)
    vmem = pl.BlockSpec(memory_space=pltpu.VMEM)
    return pl.pallas_call(
        kernel,
        out_shape=jax.ShapeDtypeStruct(hidden_in.shape, BF16),
        in_specs=[anys] * 4 + [smem] * 2 + [anys] * 8,
        out_specs=vmem,
        scratch_shapes=list(scratch.values()),
        compiler_params=pltpu.CompilerParams(collective_id=0, has_side_effects=True),
        name="layer",
    )(
        queries, new_kv, prefix_kv, decode_kv, prefix_len, decode_len, out_proj, hidden_in, expert_ids.T,
        norm_gain.reshape(1, -1), router_w.T, w_gate, w_up, w_down,
    )


def solution(mesh):
    split = Mesh(
        mesh.devices.reshape(mesh.shape["rep"], mesh.shape["exp"], mesh.shape["ten"] // 2, 2),
        ("rep", "exp", "ten_0", "ten_1"),
    )
    return jax.shard_map(
        on_device,
        mesh=split,
        in_specs=(
            P(REP_EXP_TEN, None),
            P(REP_EXP_TEN, None),
            P(None, REP_EXP_TEN, None),
            P(None, ("rep", "exp"), TEN, None),
            P(None, REP_EXP_TEN, None, None),
            P(("rep", "exp")),
            P(REP_EXP_TEN),
            P(TEN, None),
            P(),
            P(),
            P(REP_EXP_TEN, None),
            P("exp", None, TEN),
            P("exp", None, TEN),
            P("exp", TEN, None),
        ),
        out_specs=P(REP_EXP_TEN, None),
        check_vma=False,
    )
```

profile of v0, /device:TPU:513, one launch (start us, length us, event | category | flops | bytes accessed | tf_op | source)
XLA Modules:
  0.0 140.1 jit_solution(3358966122753736673)
XLA Ops:
  0.7 137.8 %layer.1 = bf16[24,3072]{1,0:T(8,128)(2,1)} custom-call(bf16[24,6144]{1,0:T(8,128)(2,1)} %q.1, bf16[2,24,1024]{2,1,0:T(8,128)(2,1)} %nkv.1, bf16[2,1,32,1024]{3,2,1,0:T(8,128)(2,1)} %pre.1, bf16[2,4,48,1024]{3,2,1,0:T(8,128)(2,1)} %dec.1, s32[1]{0:T(128)S(6)} %copy.16.plen, s32[4]{0:T(128)} %dlen.1, bf16[384,3072]{1,0:T(8,128)(2,1)} %wo.1, ...), custom_call_target="tpu_custom_call" | custom-call | tf_op jit(solution)/shard_map/layer/pallas_call | solution.py:787
  138.5 1.6 %copy.17 = bf16[24,3072]{1,0:T(8,128)(2,1)} copy(bf16[24,3072]{1,0:T(8,128)(2,1)} %layer.1) | data formatting | bytes 294912
where the time goes:
time: 140 us
  Pallas kernels  138 us (99%)
  local copies, waits for them, and re-layouts  1.58 us (1%)
    pallas_call x1, Pallas kernels, on_device(): pl.pallas_call(kernel, out_shape=jax.ShapeDtypeStruct(hidden_in.shape, BF...  138 us

commit v1 on v0

--- a/solution.py
+++ b/solution.py
@@ -13,7 +13,8 @@
 BF16 = jnp.bfloat16
 NEG = -1e30
 CHUNKS = 6
-RING_WIRE, RING_TURN, RING_SPREAD = 1.25, 2.2, 4.5
+PIECES = 12
+RING_WIRE, RING_TURN, RING_SPREAD, RING_LATE = 1.25, 3.2, 5.0, 2.0
 EXP, CHIP, CORE = "exp", "ten_0", "ten_1"
 TEN = (CHIP, CORE)
 REP_EXP_TEN = ("rep", EXP, CHIP, CORE)
@@ -47,11 +48,12 @@
     return order + [(True, 1)]
 
 
-def ring_schedule(chips, subs, wire, turn, spread):
+def ring_schedule(chips, subs, wire, turn, spread, late):
     order = ring_order(chips)
     place = {m: i for i, m in enumerate(order)}
     arrive, clock = {}, 0.0
     for index in (0, 1):
+        clock = max(clock, 4.0 * index)
         for sub in range(subs):
             clock += wire
             arrive[index, sub] = clock + turn
@@ -71,7 +73,7 @@
         arrive[pick] = clock + turn
     last = [place[True, 1], place[False, 1]]
     for sub in range(subs):
-        steps.append((max(arrive[i, sub] for i in last), 1, 0, sub))
+        steps.append((max(arrive[i, sub] for i in last) + late, 1, 0, sub))
     return [step[1:] for step in sorted(steps)]
 
 
@@ -164,23 +166,23 @@
         nkv_v=v((2, r, d["kvw"]), BF16),
         pre_v=v((2, d["pre_dev"], d["kvw"]), BF16),
         dec_v=v((2, d["dec"], d["ctx"], d["kvw"]), BF16),
-        qb=v((n, r, jw), BF16),
+        qb=v((n, r - 8, jw), BF16),
+        plen_v=v((1, 1), jnp.int32),
         kvn=v((2, c, 2, r, HD), BF16),
         kvp=v((2, c, 2, d["pre_dev"], HD), BF16),
-        dec_o=v((d["heads_q"] * 8, HD), BF16),
-        decs=v((n, 16, HD), BF16),
-        decr=v((n, 16, HD), BF16),
+        decs=v((n, 8 * d["heads_dev"], HD), BF16),
+        decr=v((n, 8 * d["heads_dev"], HD), BF16),
         qh=v((d["heads_dev"] * n * r, HD), BF16),
         kall=v((n * (d["pre_dev"] + r), HD), BF16),
         vall=v((n * (d["pre_dev"] + r), HD), BF16),
         att=v((n * r, 2 * jw), BF16),
         wo=v((2 * jw, half), BF16),
         part=v((n * r, half), F32),
-        rs_out=v((2, msgs, CHUNKS // 2, 2 * r, half // CHUNKS), BF16),
-        rs_in=v((2, msgs, CHUNKS // 2, 2 * r, half // CHUNKS), BF16),
-        l_sem=dma((8,)),
+        rs_out=v((2, msgs, PIECES // 2, 2 * r, half // PIECES), BF16),
+        rs_in=v((2, msgs, PIECES // 2, 2 * r, half // PIECES), BF16),
+        l_sem=dma((9,)),
         qs_sem=dma((1,)),
-        qr_sem=dma((1,)),
+        qr_sem=dma((2,)),
         kns_sem=dma((1,)),
         knr_sem=dma((1,)),
         kps_sem=dma((1,)),
@@ -190,7 +192,7 @@
         ds_sem=dma((1,)),
         dr_sem=dma((1,)),
         rs_s=dma((1,)),
-        rs_r=dma((msgs, CHUNKS // 2)),
+        rs_r=dma((msgs, PIECES // 2)),
     )
 
 
@@ -209,14 +211,16 @@
         return copy
 
     kv_cols = cols(y * HD, HD)
+    turn = ring_turns(c)
     l_n = local(nkv_hbm, S["nkv_v"], 0)
     l_p = local(pre_hbm.at[:, 0], S["pre_v"], 1)
     l_q = local(q_hbm, S["q_v"], 2)
     l_own = [
         local(nkv_hbm.at[:, :, kv_cols], S["kvn"].at[k, y], 3),
         local(pre_hbm.at[:, 0, :, kv_cols], S["kvp"].at[k, y], 4),
-        local(q_hbm.at[:, cols(t * jw, jw)], S["qb"].at[t], 5),
+        local(q_hbm.at[: r - 8, cols(t * jw, jw)], S["qb"].at[t], 5),
     ]
+    l_len = local(plen, S["plen_v"], 8)
     l_d = local(dec_hbm, S["dec_v"], 6)
     l_w = local(wo_hbm.at[:, cols(k * half, half)], S["wo"].at[rows(k * jw, jw, 16)], 7)
 
@@ -234,10 +238,10 @@
             S["kps_sem"].at[0], S["kpr_sem"].at[0], **{CHIP: to},
         )
 
-    def q_copy(src_t, to_t):
+    def q_copy(src_t, to_t, late):
         return remote(
-            S["q_v"].at[:, cols(to_t * jw, jw)], S["qb"].at[src_t],
-            S["qs_sem"].at[0], S["qr_sem"].at[0], **{CHIP: to_t // 2, CORE: to_t % 2},
+            S["q_v"].at[: r - 8, cols(to_t * jw, jw)], S["qb"].at[src_t],
+            S["qs_sem"].at[0], S["qr_sem"].at[late], **{CHIP: to_t // 2, CORE: to_t % 2},
         )
 
     l_n.wait()
@@ -266,6 +270,7 @@
     for i in range(1, dec):
         length = jnp.where(req == i, dlen[i], length)
     seen = (row8 - (8 - dec) == req) & (pos < length)
+    late_row = (iota((m, 1), 0) & 7) >= 8 - dec
     for g in range(hq // per_kv):
         qg = jnp.concatenate(
             [q8[:, (g * per_kv + h) * HD : (g * per_kv + h + 1) * HD] for h in range(per_kv)], axis=0
@@ -281,14 +286,7 @@
         p_own = jnp.exp(s_own - top)
         den = jnp.sum(p, axis=1, keepdims=True) + p_own
         o = dot(p.astype(BF16), vg) + p_own.astype(BF16).astype(F32) * own_v
-        S["dec_o"][g * m : (g + 1) * m, :] = (o / den).astype(BF16)
-    to_row = iota((n * 16, hq * 8), 0)
-    from_row = iota((n * 16, hq * 8), 1)
-    slot = to_row & 15
-    wanted = (to_row >> 4) * (8 * hd_dev) + (slot >> 2) * 8 + (8 - dec) + (slot & 3)
-    pick = ((from_row == wanted) & (slot < hd_dev * dec)).astype(BF16)
-    S["decs"][...] = dot(pick, S["dec_o"][...]).astype(BF16).reshape(n, 16, HD)
-
+        S["decs"][g * 2 : (g + 1) * 2] = jnp.where(late_row, o / den, qg).astype(BF16).reshape(2, m // 2, HD)
     def d_copy(src_t, to_t):
         return remote(
             S["decs"].at[to_t], S["decr"].at[src_t],
@@ -301,7 +299,8 @@
     for o in near_first(c)[::-1] + [0]:
         to = lax.rem(y + o, c)
         for kk in ([1] if o == 0 else [0, 1]):
-            copies.start(q_copy(t, 2 * to + lax.rem(k + kk, 2)))
+            late = int(turn.index((c - o) % c) >= c // 2)
+            copies.start(q_copy(t, 2 * to + lax.rem(k + kk, 2), late))
 
     for copy in l_own:
         copy.wait()
@@ -315,15 +314,7 @@
         copies.start(remote(S[b].at[k], S[b].at[k], S["x_s"].at[i], S["x_r"].at[i], **{CORE: other}))
         for i, b in ((1, "kvn"), (2, "kvp"))
     ]
-    arrived(S["qb"].at[: n - 1], S["qr_sem"].at[0])
-    turn = ring_turns(c)
     chip_at = [lax.rem(y + o, c) for o in turn]
-    for cc in range(c):
-        pair = [S["qb"][2 * chip_at[cc] + i].astype(F32) for i in range(2)]
-        for j in range(hd_dev):
-            S["qh"][j * n * r + cc * 2 * r : j * n * r + (cc + 1) * 2 * r, :] = jnp.concatenate(
-                [q[:, j * HD : (j + 1) * HD] for q in pair], axis=0
-            ).astype(BF16)
     for copy in relay:
         copy.wait()
     prefix = n * pre_dev
@@ -343,13 +334,27 @@
     col_dev = sum((col >= r * i).astype(jnp.int32) for i in range(1, n))
     col_in = col - r * col_dev
     key_place = jnp.where(col_in < span, col_dev * span + col_in, 1 << 20)
-    pre_seen = iota((1, prefix), 1) < plen[0]
+    l_len.wait()
+    pre_seen = iota((1, prefix), 1) < S["plen_v"][...]
     row = iota((block, 1), 0)
     row_dev = sum((row >= r * i).astype(jnp.int32) for i in range(1, block_devs))
     row_in = row - r * row_dev
-    from_col = iota((block, n * 16), 1)
+    blank = jnp.zeros((r - 8, HD), F32)
     att_copies = []
     for b in range(n // block_devs):
+        arrived(S["qb"].at[: block_devs - b], S["qr_sem"].at[b])
+        for cc in range(b * c // 2, (b + 1) * c // 2):
+            pair = [2 * chip_at[cc] + i for i in range(2)]
+            body = [S["qb"][device].astype(F32) for device in pair]
+            for j in range(hd_dev):
+                S["qh"][j * n * r + cc * 2 * r : j * n * r + (cc + 1) * 2 * r, :] = jnp.concatenate(
+                    [
+                        piece
+                        for device, q in zip(pair, body)
+                        for piece in (q[:, j * HD : (j + 1) * HD], S["decr"][device, 8 * j : 8 * j + 8].astype(F32))
+                    ],
+                    axis=0,
+                ).astype(BF16)
         chip = sum(
             jnp.where((row_dev >> 1) == i, chip_at[b * block_devs // 2 + i], 0) for i in range(block_devs // 2)
         )
@@ -365,8 +370,15 @@
             p2 = jnp.exp((s2 - top) * scale)
             den = jnp.sum(p1, axis=1, keepdims=True) + jnp.sum(p2, axis=1, keepdims=True)
             o = (dot(p1.astype(BF16), S["vall"][:prefix, :]) + dot(p2.astype(BF16), S["vall"][prefix:, :])) / den
-            wanted = jnp.where(row_in >= span, device * 16 + j * dec + row_in - span, -1)
-            own = dot((from_col == wanted).astype(BF16), S["decr"][...].reshape(n * 16, HD))
+            own = jnp.concatenate(
+                [
+                    piece
+                    for at in chip_at[b * c // 2 : (b + 1) * c // 2]
+                    for i in range(2)
+                    for piece in (blank, S["decr"][2 * at + i, 8 * j : 8 * j + 8].astype(F32))
+                ],
+                axis=0,
+            )
             S["att"][first : first + block, cols(k * jw + j * HD, HD)] = jnp.where(
                 row_in < span, o, own
             ).astype(BF16)
@@ -377,7 +389,7 @@
     l_w.wait()
     wo_copy.wait()
 
-    width, subs = half // CHUNKS, CHUNKS // 2
+    width, subs, wide = half // PIECES, PIECES // 2, PIECES // CHUNKS
     row_of = {o: i * 2 * r for i, o in enumerate(turn)}
 
     def share(o, h, sub):
@@ -388,16 +400,17 @@
     for b, copy in enumerate(att_copies):
         copy.wait()
         these = slice(b * block, (b + 1) * block)
-        for sub in range(subs):
+        for sub in range(0, subs, wide):
             for h in range(2):
                 first = (h * subs + sub) * width
-                S["part"][these, first : first + width] = dot(
-                    S["att"][these, :], S["wo"][:, first : first + width]
+                S["part"][these, first : first + wide * width] = dot(
+                    S["att"][these, :], S["wo"][:, first : first + wide * width]
                 )
                 if b == 0:
-                    ring.first(0, sub, 1 - h)
-                    ring.first(1, sub, h)
-    for index in range(2, len(ring.order)):
+                    for s in range(sub, sub + wide):
+                        ring.first(1, s, h)
+                        ring.first(0, s, 1 - h)
+    for index in sorted(range(2, len(ring.order)), key=lambda i: -(2 * ring.order[i][1] + (not ring.order[i][0]))):
         for sub in range(subs):
             ring.send(index, sub)
     sums = [ring.totals(sub) for sub in range(subs)]
@@ -446,6 +459,7 @@
         xg=v((2, c, groups * take, half), BF16),
         hid=v((2, c * groups * take, ff), BF16),
         part2=v((c * groups * take, half), F32),
+        gu=v((2, 2 * groups * take, ff), F32),
         rs2_out=v((2, msgs, nq // 2, groups * take, half // nq), BF16),
         rs2_in=v((2, msgs, nq // 2, groups * take, half // nq), BF16),
         ys=v((groups, slots, half), BF16),
@@ -537,35 +551,43 @@
         for i in (0, 4, 5):
             self.loads[i].wait()
 
-    def ffn_gate_up(self, offs, tile):
+    def ffn_gate_up(self, offs, mine):
         S, d = self.S, self.d
-        half, n = d["model"] // 2, d["groups"] * 2 * CAP
-        width = d["ff_dev"] // 2
-        at = slice(tile * width, (tile + 1) * width)
-        xh = [jnp.concatenate([S["xg"][h, self.chip(o)] for o in offs], axis=0) for h in range(2)]
-        gate = dot(xh[0], S["wg"][:half, at]) + dot(xh[1], S["wg"][half:, at])
-        up = dot(xh[0], S["wu"][:half, at]) + dot(xh[1], S["wu"][half:, at])
-        act = (gate / (1.0 + jnp.exp(-gate)) * up).astype(BF16)
-        for i, o in enumerate(offs):
-            S["hid"][self.k, rows(self.chip(o) * n, n, 16), at] = act[i * n : (i + 1) * n]
+        half, n, width = d["model"] // 2, d["groups"] * 2 * CAP, d["ff_dev"] // 2
+        h = self.k if mine else 1 - self.k
+        lhs = jnp.concatenate([S["xg"][h, self.chip(o)] for o in offs], axis=0)
+        some = slice(0, len(offs) * n)
+        for tile in range(2):
+            at = slice(tile * width, (tile + 1) * width)
+            gate = dot(lhs, S["wg"][rows(h * half, half, 16), at])
+            up = dot(lhs, S["wu"][rows(h * half, half, 16), at])
+            if mine:
+                S["gu"][0, some, at] = gate
+                S["gu"][1, some, at] = up
+                continue
+            gate = gate + S["gu"][0, some, at]
+            up = up + S["gu"][1, some, at]
+            act = (gate / (1.0 + jnp.exp(-gate)) * up).astype(BF16)
+            for i, o in enumerate(offs):
+                S["hid"][self.k, rows(self.chip(o) * n, n, 16), at] = act[i * n : (i + 1) * n]
 
     def hid_copy(self, o):
         n = self.d["groups"] * 2 * CAP
         view = self.S["hid"].at[self.k, rows(self.chip(o) * n, n, 16)]
         return remote(view, view, self.S["h_s"].at[0], self.S["h_r"].at[self.away(o)], **{CORE: 1 - self.k})
 
-    def ffn_down(self, offs, after=None):
+    def ffn_down(self, offs, mine, after=None):
         S, d = self.S, self.d
         half, n = d["model"] // 2, d["groups"] * 2 * CAP
-        lhs = [
-            jnp.concatenate([S["hid"][h, rows(self.chip(o) * n, n, 16), :] for o in offs], axis=0)
-            for h in range(2)
-        ]
+        h = self.k if mine else 1 - self.k
+        lhs = jnp.concatenate([S["hid"][h, rows(self.chip(o) * n, n, 16), :] for o in offs], axis=0)
 
         def tile(at):
-            value = dot(lhs[0], S["wd"][0, :, at]) + dot(lhs[1], S["wd"][1, :, at])
+            value = dot(lhs, S["wd"][h, :, at])
             for j, o in enumerate(offs):
-                S["part2"][rows(self.chip(o) * n, n, 16), at] = value[j * n : (j + 1) * n]
+                place = rows(self.chip(o) * n, n, 16)
+                more = value[j * n : (j + 1) * n]
+                S["part2"][place, at] = more if mine else S["part2"][place, at] + more
 
         def step(i, carry):
             tile(cols(i * 256, 256))
@@ -576,23 +598,24 @@
             lax.fori_loop(0, half // 256, step, 0)
         else:
             for sub in range(subs):
-                for h in range(2):
-                    first = (h * subs + sub) * width
+                for half_of in range(2):
+                    first = (half_of * subs + sub) * width
                     tile(slice(first, first + width))
-                    after(h, sub)
+                    after(half_of, sub)
 
     def ffn(self, offs, stage, after=None):
         if stage == 0:
+            self.ffn_gate_up(offs, True)
+        elif stage == 1:
             arrived(self.S["xg"].at[0, : len(offs)], self.S["pc_r"].at[self.away(offs[0])])
-            self.ffn_gate_up(offs, 0)
-        elif stage == 1:
-            self.ffn_gate_up(offs, 1)
+            self.ffn_gate_up(offs, False)
             for o in offs:
                 self.copies.start(self.hid_copy(o))
-        elif stage == CHUNKS - 1:
+        elif stage == 3:
+            self.ffn_down(offs, True)
             n = self.d["groups"] * 2 * CAP
             arrived(self.S["hid"].at[0, : len(offs) * n], self.S["h_r"].at[self.away(offs[0])])
-            self.ffn_down(offs, after)
+            self.ffn_down(offs, False, after)
 
     def chunk(self, q):
         w = self.d["model"] // 2 // CHUNKS
@@ -688,13 +711,18 @@
 
         ring = RingSum(y, c, copies, share, S["rs2_out"], S["rs2_in"], S["rs2_s"], S["rs2_r"], subs)
         blocks = [[0]] + [[c - s, s] for s in range(1, far)] + [[far]]
-        for hop in range(1, far + 1):
+        for hop in range(1, far):
             for q in range(CHUNKS):
                 if hop > 1 or q >= CHUNKS - ahead:
                     pass_on(hop, q)
-                self.ffn(
-                    blocks[hop - 1], q, None if hop < far else lambda h, sub: ring.first(0, sub, 1 - h)
-                )
+                self.ffn(blocks[hop - 1], q)
+        self.ffn(blocks[far - 1], 0)
+        for q in range(CHUNKS // 2):
+            pass_on(far, q)
+        self.ffn(blocks[far - 1], 1)
+        for q in range(CHUNKS // 2, CHUNKS):
+            pass_on(far, q)
+        self.ffn(blocks[far - 1], 3, lambda h, sub: ring.first(0, sub, 1 - h))
         for stage in range(CHUNKS):
             self.ffn(blocks[far], stage, lambda h, sub: ring.first(1, sub, h))
 
@@ -708,7 +736,7 @@
         w_lo = (weight - w_hi.astype(F32)).astype(BF16)
         ja, jb = iota((128, n), 0), iota((128, n), 1)
         spread = (((ja >> 4) * (2 * CAP) + (ja & 15) == jb) & ((ja & 15) < 2 * CAP)).astype(BF16)
-        for kind, index, sub in ring_schedule(c, subs, RING_WIRE, RING_TURN, RING_SPREAD):
+        for kind, index, sub in ring_schedule(c, subs, RING_WIRE, RING_TURN, RING_SPREAD, RING_LATE):
             if kind == 0:
                 ring.send(index, sub)
                 continue
@@ -732,7 +760,7 @@
             copies.start(back(q))
         arrived(S["fin"].at[1 - k, rows(k * r, r, 8), :], S["f_r"].at[0])
         for h in range(2):
-            self.out[:, h * half : (h + 1) * half] = S["fin"][h, rows(k * r, r, 8), :].astype(BF16)
+            self.out[:, h * half : (h + 1) * half] = S["fin"][h, rows(k * r, r, 8), :]
         copies.sent(S["xs"].at[: groups - 1], S["xs_s"].at[0])
         copies.sent(S["ys"].at[: groups - 1], S["ys_s"].at[0])
         copies.sent(S["xg"].at[0, : c - 1], S["ag_s"].at[0])
@@ -786,16 +814,16 @@
     vmem = pl.BlockSpec(memory_space=pltpu.VMEM)
     return pl.pallas_call(
         kernel,
-        out_shape=jax.ShapeDtypeStruct(hidden_in.shape, BF16),
-        in_specs=[anys] * 4 + [smem] * 2 + [anys] * 8,
+        out_shape=jax.ShapeDtypeStruct(hidden_in.shape, F32),
+        in_specs=[anys] * 5 + [smem] + [anys] * 8,
         out_specs=vmem,
         scratch_shapes=list(scratch.values()),
         compiler_params=pltpu.CompilerParams(collective_id=0, has_side_effects=True),
         name="layer",
     )(
-        queries, new_kv, prefix_kv, decode_kv, prefix_len, decode_len, out_proj, hidden_in, expert_ids.T,
+        queries, new_kv, prefix_kv, decode_kv, prefix_len.reshape(1, 1), decode_len, out_proj, hidden_in, expert_ids.T,
         norm_gain.reshape(1, -1), router_w.T, w_gate, w_up, w_down,
-    )
+    ).astype(BF16)
 
 
 def solution(mesh):

time: 140 us -> 136 us (0.971)
  Pallas kernels: 138 us -> 134 us
  other arithmetic: 0 us -> 1.64 us
  local copies, waits for them, and re-layouts: 1.58 us -> 0 us
    pallas_call x1, Pallas kernels: 138 us -> 134 us  [on_device(): pl.pallas_call(kernel, out_shape=jax.ShapeDtypeStruct(hidden_in.shape, F3...]
    convert_element_type x0 -> x1, other arithmetic: none -> 1.64 us  [on_device(): return pl.pallas_call(kernel, out_shape=jax.ShapeDtypeStruct(hidden_in.sh...]
    unnamed x1 -> x0, local copies, waits for them, and re-layouts: 1.58 us -> none
where the time goes in v1:
time: 136 us
  Pallas kernels  134 us (99%)
  other arithmetic  1.64 us (1%)
    pallas_call x1, Pallas kernels, on_device(): pl.pallas_call(kernel, out_shape=jax.ShapeDtypeStruct(hidden_in.shape, F3...  134 us

profile of v1, /device:TPU:513, one launch (start us, length us, event | category | flops | bytes accessed | tf_op | source)
XLA Modules:
  0.0 136.2 jit_solution(1397830445419423648)
XLA Ops:
  0.7 133.9 %layer.1 = f32[24,3072]{1,0:T(8,128)} custom-call(bf16[24,6144]{1,0:T(8,128)(2,1)} %q.1, bf16[2,24,1024]{2,1,0:T(8,128)(2,1)} %nkv.1, bf16[2,1,32,1024]{3,2,1,0:T(8,128)(2,1)} %pre.1, bf16[2,4,48,1024]{3,2,1,0:T(8,128)(2,1)} %dec.1, s32[1,1]{1,0:T(1,128)} %bitcast.4.plen, s32[4]{0:T(128)} %dlen.1, bf16[384,3072]{1,0:T(8,128)(2,1)} %wo.1, ...), custom_call_target="tpu_custom_call" | custom-call | tf_op jit(solution)/shard_map/layer/pallas_call | solution.py:815
  134.5 1.6 %convert_element_type.3 = bf16[24,3072]{1,0:T(8,128)(2,1)} convert(f32[24,3072]{1,0:T(8,128)} %layer.1) | non-fusion elementwise | flops 73728 | bytes 442368 | tf_op jit(solution)/shard_map/convert_element_type | solution.py:826

commit v2 on v1

--- a/solution.py
+++ b/solution.py
@@ -717,12 +717,10 @@
                     pass_on(hop, q)
                 self.ffn(blocks[hop - 1], q)
         self.ffn(blocks[far - 1], 0)
-        for q in range(CHUNKS // 2):
+        self.ffn(blocks[far - 1], 1)
+        self.ffn(blocks[far - 1], 3, lambda h, sub: ring.first(0, sub, 1 - h))
+        for q in range(CHUNKS):
             pass_on(far, q)
-        self.ffn(blocks[far - 1], 1)
-        for q in range(CHUNKS // 2, CHUNKS):
-            pass_on(far, q)
-        self.ffn(blocks[far - 1], 3, lambda h, sub: ring.first(0, sub, 1 - h))
         for stage in range(CHUNKS):
             self.ffn(blocks[far], stage, lambda h, sub: ring.first(1, sub, h))
 
@@ -760,7 +758,7 @@
             copies.start(back(q))
         arrived(S["fin"].at[1 - k, rows(k * r, r, 8), :], S["f_r"].at[0])
         for h in range(2):
-            self.out[:, h * half : (h + 1) * half] = S["fin"][h, rows(k * r, r, 8), :]
+            self.out[:, h * half : (h + 1) * half] = S["fin"][h, rows(k * r, r, 8), :].astype(BF16)
         copies.sent(S["xs"].at[: groups - 1], S["xs_s"].at[0])
         copies.sent(S["ys"].at[: groups - 1], S["ys_s"].at[0])
         copies.sent(S["xg"].at[0, : c - 1], S["ag_s"].at[0])
@@ -814,7 +812,7 @@
     vmem = pl.BlockSpec(memory_space=pltpu.VMEM)
     return pl.pallas_call(
         kernel,
-        out_shape=jax.ShapeDtypeStruct(hidden_in.shape, F32),
+        out_shape=jax.ShapeDtypeStruct(hidden_in.shape, BF16),
         in_specs=[anys] * 5 + [smem] + [anys] * 8,
         out_specs=vmem,
         scratch_shapes=list(scratch.values()),
@@ -823,7 +821,7 @@
     )(
         queries, new_kv, prefix_kv, decode_kv, prefix_len.reshape(1, 1), decode_len, out_proj, hidden_in, expert_ids.T,
         norm_gain.reshape(1, -1), router_w.T, w_gate, w_up, w_down,
-    ).astype(BF16)
+    )
 
 
 def solution(mesh):

time: 136 us -> 135 us (level)
  other arithmetic: 1.64 us -> 0 us
  local copies, waits for them, and re-layouts: 0 us -> 1.58 us
    convert_element_type x1 -> x0, other arithmetic: 1.64 us -> none  [on_device(): return pl.pallas_call(kernel, out_shape=jax.ShapeDtypeStruct(hidden_in.sh...]
    unnamed x0 -> x1, local copies, waits for them, and re-layouts: none -> 1.58 us
where the time goes in v2:
time: 135 us
  Pallas kernels  133 us (99%)
  local copies, waits for them, and re-layouts  1.58 us (1%)
    pallas_call x1, Pallas kernels, on_device(): pl.pallas_call(kernel, out_shape=jax.ShapeDtypeStruct(hidden_in.shape, BF...  133 us

profile of v2, /device:TPU:513, one launch (start us, length us, event | category | flops | bytes accessed | tf_op | source)
XLA Modules:
  0.0 135.3 jit_solution(12236646824677127352)
XLA Ops:
  0.7 133.1 %layer.1 = bf16[24,3072]{1,0:T(8,128)(2,1)} custom-call(bf16[24,6144]{1,0:T(8,128)(2,1)} %q.1, bf16[2,24,1024]{2,1,0:T(8,128)(2,1)} %nkv.1, bf16[2,1,32,1024]{3,2,1,0:T(8,128)(2,1)} %pre.1, bf16[2,4,48,1024]{3,2,1,0:T(8,128)(2,1)} %dec.1, s32[1,1]{1,0:T(1,128)} %bitcast.4.plen, s32[4]{0:T(128)} %dlen.1, bf16[384,3072]{1,0:T(8,128)(2,1)} %wo.1, ...), custom_call_target="tpu_custom_call" | custom-call | tf_op jit(solution)/shard_map/layer/pallas_call | solution.py:813
  133.7 1.6 %copy.17 = bf16[24,3072]{1,0:T(8,128)(2,1)} copy(bf16[24,3072]{1,0:T(8,128)(2,1)} %layer.1) | data formatting | bytes 294912
